TPU v7x, 32 devices: a whole 2x2x4 slice. The times are simulated.
32 devices in a mesh: lat: 4 (over y, x), lon: 8 (over z, core).
Axes of the slice: x: 2, y: 2, z: 4, core: 2. Of those that a mesh axis runs over, the one named last changes fastest.
Arguments:
- atmos_features: bfloat16 [128, 256, 768], P('lat', 'lon'), may hold values from -6 to 6
- ocean_features: bfloat16 [256, 512, 192], P('lat', 'lon'), may hold values from -6 to 6
- wet_cell_mask: int32 [256, 512], P('lat', 'lon'), may hold values from 0 to 1, as said below
- overlay_cell_index: int32 [4, 256, 512], P(None, 'lat', 'lon'), may hold values from 0 to 8191, as said below
- remap_weight: float32 [4, 256, 512], P(None, 'lat', 'lon'), may hold values from 0.1 to 1
- query_key_value_weight: bfloat16 [768, 2304], replicated, may hold values from -5 to 5
- attention_out_weight: bfloat16 [768, 768], replicated, may hold values from -0.21875 to 0.21875
- feedforward_up_weight: bfloat16 [768, 3072], replicated, may hold values from -0.21875 to 0.21875
- feedforward_down_weight: bfloat16 [3072, 768], replicated, may hold values from -0.109375 to 0.109375
- attention_gain: float32 [768], replicated, may hold values from 0.25 to 1.75
- feedforward_gain: float32 [768], replicated, may hold values from 0.25 to 1.75
- flux_head_weight: bfloat16 [768, 8], replicated, may hold values from -0.21875 to 0.21875
- surface_temp_embedding: float32 [768], replicated, may hold values from -5 to 5
- forcing_lift_weight: float32 [8, 192], replicated, may hold values from -2 to 2
- depthwise_kernels: float32 [2, 49, 192], replicated, may hold values from -0.875 to 0.875
- ocean_norm_gains: float32 [2, 192], replicated, may hold values from 0.25 to 1.75
- ocean_up_weights: bfloat16 [2, 192, 768], replicated, may hold values from -0.4375 to 0.4375
- ocean_down_weights: bfloat16 [2, 768, 192], replicated, may hold values from -0.21875 to 0.21875
- surface_temp_head: float32 [192], replicated, may hold values from -0.4375 to 0.4375
Outputs:
- atmos_updated: bfloat16 [128, 256, 768], P('lat', 'lon')
- ocean_out: bfloat16 [256, 512, 192], P('lat', 'lon')
Inputs may be any that keep to these rules, and one draw needn't show every extreme that they name: `wet_cell_mask`: the ocean tile of rows [i * 64, i * 64 + 64) and columns [j * 64, j * 64 + 64) and the tile 256 / 2 rows north or south of it in the same columns together hold at most 4096 wet cells; some pair holds exactly that many. `overlay_cell_index`: each entry names an atmosphere cell of the latitude band of the ocean row: ocean row r belongs to the band of atmosphere rows [(r // 64) * 32, (r // 64) * 32 + 32), and the entry is (row within the band) * 256 + column.
All inputs are finite; a program needn't handle non-finite values.
Results may differ from a plain program's by a relative error of at most 0.013.
Values may be sent and summed in bfloat16 or wider, within the bound.
No kernel may reach another device: no remote copies, remote signals or barrier semaphores. Data moves between devices by JAX's collectives and lax.ppermute only.
A program may use at most 128 MiB of HBM per device.

v0:
```python
import jax
import jax.numpy as jnp
from jax import lax
from jax.sharding import PartitionSpec as P

HEADS = 12
HD = 64
WR = 8
WC = 16


EPS = 1e-06


def with_halo(block, sides, width):
    for axis, dim in sides:
        count = lax.axis_size(axis)
        forward = [(i, i + 1) for i in range(count - 1)]
        forward.append((count - 1, 0))
        backward = [(target, source) for source, target in forward]
        low = lax.ppermute(
            lax.slice_in_dim(block, block.shape[dim] - width, None, axis=dim), axis, forward
        )
        high = lax.ppermute(lax.slice_in_dim(block, 0, width, axis=dim), axis, backward)
        block = jnp.concatenate([low, block, high], axis=dim)
    return block


def swapped(block, axis, apart):
    count = lax.axis_size(axis)
    route = []
    for low in range(count):
        high = low | 1 << apart
        if high != low and high < count:
            route += [(low, high), (high, low)]
    return lax.ppermute(block, axis, route)


def rms_scale(values, gain):
    return values * lax.rsqrt(jnp.mean(values * values, axis=-1, keepdims=True) + EPS) * gain


def layer_scale(values, gain):
    center = values - jnp.mean(values, axis=-1, keepdims=True)
    return center * lax.rsqrt(jnp.mean(center * center, axis=-1, keepdims=True) + EPS) * gain


def to_windows(tensor):
    row_total, column_total = (tensor.shape[0], tensor.shape[1])
    shaped = tensor.reshape(row_total // WR, WR, column_total // WC, WC, HEADS, HD)
    return shaped.transpose(0, 2, 4, 1, 3, 5).reshape(-1, HEADS, WR * WC, HD)


def from_windows(tensor, row_total, column_total):
    shaped = tensor.reshape(row_total // WR, column_total // WC, HEADS, WR, WC, HD)
    return shaped.transpose(0, 3, 1, 4, 2, 5).reshape(row_total, column_total, HEADS * HD)


def depthwise(padded, taps, row_total, column_total):
    total = jnp.zeros((row_total, column_total, padded.shape[2]), jnp.float32)
    for north in range(7):
        for east in range(7):
            window = padded[north : north + row_total, east : east + column_total].astype(
                jnp.float32
            )
            total = total + window * taps[north * 7 + east]
    return total


def ocean_mlp(normed, up_weight, down_weight):
    active = jax.nn.gelu(jnp.dot(normed, up_weight, preferred_element_type=jnp.float32)).astype(
        jnp.bfloat16
    )
    return jnp.dot(active, down_weight, preferred_element_type=jnp.float32)


def body(
    atmos_features,
    ocean_features,
    wet_cell_mask,
    overlay_cell_index,
    remap_weight,
    query_key_value_weight,
    attention_out_weight,
    feedforward_up_weight,
    feedforward_down_weight,
    attention_gain,
    feedforward_gain,
    flux_head_weight,
    surface_temp_embedding,
    forcing_lift_weight,
    depthwise_kernels,
    ocean_norm_gains,
    ocean_up_weights,
    ocean_down_weights,
    surface_temp_head,
):
    row_total, column_total, width = atmos_features.shape
    half_window = WC // 2
    model_state = atmos_features.astype(jnp.float32)
    normed = rms_scale(model_state, attention_gain).astype(jnp.bfloat16)
    query = jnp.dot(
        normed, query_key_value_weight[:, :width], preferred_element_type=jnp.float32
    ).astype(jnp.bfloat16)
    own_pairs = jnp.dot(
        normed, query_key_value_weight[:, width:], preferred_element_type=jnp.float32
    ).astype(jnp.bfloat16)
    key_value = with_halo(own_pairs, (("lon", 1),), half_window)
    query_wide = jnp.pad(query, ((0, 0), (half_window, half_window), (0, 0)))
    query_win = to_windows(query_wide)
    keys_win = to_windows(key_value[..., :width])
    value_win = to_windows(key_value[..., width:])
    scores = jnp.einsum(
        "whqd,whkd->whqk", query_win, keys_win, preferred_element_type=jnp.float32
    ) * HD ** (-0.5)
    probs = jax.nn.softmax(scores, axis=-1).astype(jnp.bfloat16)
    mixed = jnp.einsum(
        "whqk,whkd->whqd", probs, value_win, preferred_element_type=jnp.float32
    ).astype(jnp.bfloat16)
    attended = from_windows(mixed, row_total, column_total + WC)[
        :, half_window : half_window + column_total
    ]
    first = model_state + jnp.dot(
        attended, attention_out_weight, preferred_element_type=jnp.float32
    )
    normed_mlp = rms_scale(first, feedforward_gain).astype(jnp.bfloat16)
    active = jax.nn.gelu(
        jnp.dot(normed_mlp, feedforward_up_weight, preferred_element_type=jnp.float32)
    ).astype(jnp.bfloat16)
    second_half = first + jnp.dot(
        active, feedforward_down_weight, preferred_element_type=jnp.float32
    )
    fluxes = jnp.dot(
        second_half.astype(jnp.bfloat16), flux_head_weight, preferred_element_type=jnp.float32
    ).astype(jnp.bfloat16)
    band_flux = lax.all_gather(fluxes, "lon", axis=1, tiled=True)
    band_flat = band_flux.reshape(-1, band_flux.shape[2])
    picked = band_flat[overlay_cell_index].astype(jnp.float32)
    forcing = jnp.sum(remap_weight[..., None] * picked, axis=0)
    ocean_rows, ocean_cols, channels = ocean_features.shape
    wet = wet_cell_mask.astype(jnp.float32)[..., None]
    lifted = jnp.dot(
        forcing,
        forcing_lift_weight,
        precision=lax.Precision.HIGHEST,
        preferred_element_type=jnp.float32,
    )
    ocean_field = wet * (ocean_features.astype(jnp.float32) + lifted)
    lat_index = lax.axis_index("lat")
    lat_count = lax.axis_size("lat")
    lon_count = lax.axis_size("lon")
    for block_id in range(depthwise_kernels.shape[0]):
        rounded = ocean_field.astype(jnp.bfloat16)
        padded = with_halo(rounded, (("lat", 0), ("lon", 1)), 3)
        top_rows = padded[ocean_rows : ocean_rows + 3]
        folded = top_rows[::-1, ::-1]
        for bit_index in range(lon_count.bit_length() - 1):
            folded = swapped(folded, "lon", bit_index)
        north_rows = jnp.where(lat_index == lat_count - 1, folded, padded[ocean_rows + 3 :])
        south_rows = jnp.where(lat_index == 0, jnp.zeros_like(padded[:3]), padded[:3])
        padded = jnp.concatenate([south_rows, padded[3 : ocean_rows + 3], north_rows], axis=0)
        convolved = depthwise(padded, depthwise_kernels[block_id], ocean_rows, ocean_cols)
        normed_ocean = layer_scale(convolved, ocean_norm_gains[block_id]).astype(jnp.bfloat16)
        increment = ocean_mlp(
            normed_ocean, ocean_up_weights[block_id], ocean_down_weights[block_id]
        )
        ocean_field = ocean_field + wet * increment
    ocean_out = ocean_field.astype(jnp.bfloat16)
    sea_surface_temp = jnp.dot(
        ocean_field,
        surface_temp_head,
        precision=lax.Precision.HIGHEST,
        preferred_element_type=jnp.float32,
    )
    numerator = sea_surface_temp.reshape(row_total, 2, column_total, 2).sum(axis=(1, 3))
    wet_cell_count = (
        wet_cell_mask.reshape(row_total, 2, column_total, 2).sum(axis=(1, 3)).astype(jnp.float32)
    )
    surface_temp_atmos = numerator / jnp.maximum(wet_cell_count, 1.0)
    atmos_updated = (second_half + surface_temp_atmos[..., None] * surface_temp_embedding).astype(
        jnp.bfloat16
    )
    return (atmos_updated, ocean_out)


def solution(mesh):
    in_specs = (
        P("lat", "lon", None),
        P("lat", "lon", None),
        P("lat", "lon"),
        P(None, "lat", "lon"),
        P(None, "lat", "lon"),
        P(),
        P(),
        P(),
        P(),
        P(),
        P(),
        P(),
        P(),
        P(),
        P(),
        P(),
        P(),
        P(),
        P(),
    )
    out_specs = (P("lat", "lon", None), P("lat", "lon", None))
    return jax.shard_map(body, mesh=mesh, in_specs=in_specs, out_specs=out_specs, check_vma=False)
```

profile of v0, /device:TPU:0, one launch (start us, length us, event | category | flops | bytes accessed | tf_op | source)
XLA Modules:
  0.0 462.3 jit_solution(7482006994280381155)
XLA Ops:
  2.6 4.9 %convolution_convert_fusion = bf16[32,32,1536]{2,1,0:T(8,128)(2,1)S(1)} fusion(bf16[768,2304]{1,0:T(8,128)(2,1)} %param.24, bf16[32,32,768]{2,1,0:T(8,128)(2,1)} %param.19, f32[768]{0:T(1024)} %param.28, f32[32,32]{1,0:T(8,128)S(1)} %add_rsqrt_fusion.3), kind=kOutput, calls=%fused_computation.138 | convolution fusion | flops 2420637696 | bytes 7086080 | tf_op jit(solution)/shard_map/dot_general | solution.py:105
  9.4 4.0 collective-permute-start.1
  18.5 6.3 %reshape.289 = bf16[4,8,3,16,12,64]{5,4,3,2,1,0:T(8,128)(2,1)} reshape(bf16[32,48,768]{2,1,0:T(8,128)(2,1)S(1)} %pad.4) | data formatting | bytes 4718592 | tf_op jit(solution)/shard_map/reshape | solution.py:50
  24.8 6.4 %copy.36 = bf16[4,3,12,8,16,64]{5,4,3,2,1,0:T(8,128)(2,1)} copy(bf16[4,3,12,8,16,64]{5,2,4,1,3,0:T(8,128)(2,1)} %bitcast.176) | data formatting | bytes 4718592 | tf_op jit(solution)/shard_map/transpose | solution.py:51
  38.4 8.2 %reshape.291 = bf16[4,8,3,16,12,64]{5,4,3,2,1,0:T(8,128)(2,1)} reshape(bf16[32,48,768]{2,1,0:T(8,128)(2,1)} %get-tuple-element.6) | data formatting | bytes 4718592 | tf_op jit(solution)/shard_map/reshape | solution.py:50
  46.6 6.3 %copy.37 = bf16[4,3,12,8,16,64]{5,4,3,2,1,0:T(8,128)(2,1)} copy(bf16[4,3,12,8,16,64]{5,2,4,1,3,0:T(8,128)(2,1)} %bitcast.177) | data formatting | bytes 4718592 | tf_op jit(solution)/shard_map/transpose | solution.py:51
  52.9 5.9 %reshape.293 = bf16[4,8,3,16,12,64]{5,4,3,2,1,0:T(8,128)(2,1)} reshape(bf16[32,48,768]{2,1,0:T(8,128)(2,1)S(1)} %get-tuple-element.7) | data formatting | bytes 4718592 | tf_op jit(solution)/shard_map/reshape | solution.py:50
  58.8 6.3 %copy.40 = bf16[4,3,12,8,16,64]{5,4,3,2,1,0:T(8,128)(2,1)} copy(bf16[4,3,12,8,16,64]{5,2,4,1,3,0:T(8,128)(2,1)} %bitcast.178) | data formatting | bytes 4718592 | tf_op jit(solution)/shard_map/transpose | solution.py:51
  65.1 11.8 %fusion.206 = (f32[12,12,128]{2,1,0:T(8,128)}, f32[12,12,128,128]{2,3,1,0:T(8,128)}) fusion(bf16[12,12,128,64]{3,2,1,0:T(8,128)(2,1)} %bitcast.181, bf16[12,12,128,64]{3,2,1,0:T(8,128)(2,1)} %bitcast.182), kind=kOutput, calls=%fused_computation.362 | convolution fusion | flops 309067904 | bytes 14229504 | tf_op jit(solution)/shard_map/sub | solution.py:116
  76.9 6.6 %fusion.142 = bf16[12,12,128,64]{2,3,1,0:T(8,128)(2,1)S(1)} fusion(bf16[12,12,128,64]{3,2,1,0:T(8,128)(2,1)} %bitcast.183, f32[12,12,128,128]{2,3,1,0:T(8,128)} %get-tuple-element.127, f32[12,12,128]{2,1,0:T(8,128)} %get-tuple-element.126), kind=kOutput, calls=%fused_computation.292 | convolution fusion | flops 307888128 | bytes 14229504 | tf_op jit(solution)/shard_map/whqk,whkd->whqd/dot_general | solution.py:117
  83.6 4.5 copy.43
  88.1 10.6 %copy.44 = bf16[4,8,3,16,12,64]{5,4,3,2,1,0:T(8,128)(2,1)} copy(bf16[4,8,3,16,12,64]{5,3,1,4,2,0:T(8,128)(2,1)} %bitcast.179) | data formatting | bytes 4718592 | tf_op jit(solution)/shard_map/transpose | solution.py:56
  98.7 7.2 %reshape.296 = bf16[32,48,768]{2,1,0:T(8,128)(2,1)S(1)} reshape(bf16[4,8,3,16,12,64]{5,4,3,2,1,0:T(8,128)(2,1)} %copy.44) | data formatting | bytes 4718592 | tf_op jit(solution)/shard_map/reshape | solution.py:56
  109.1 7.3 %fusion.36 = f32[32,32,3072]{2,1,0:T(8,128)S(1)} fusion(bf16[768,3072]{1,0:T(8,128)(2,1)} %param.26, f32[32,32,768]{2,1,0:T(8,128)S(1)} %get-tuple-element.129, f32[768]{0:T(1024)S(1)} %copy-done.100, f32[32,32]{1,0:T(8,128)S(1)} %add_rsqrt_fusion.2), kind=kOutput, calls=%fused_computation.123 | convolution fusion | flops 4834197504 | bytes 20454400 | tf_op jit(solution)/shard_map/dot_general | solution.py:128
  116.4 7.4 %fusion.145 = f32[32,32,768]{2,1,0:T(8,128)S(1)} fusion(f32[32,32,768]{2,1,0:T(8,128)S(1)} %get-tuple-element.129, bf16[3072,768]{1,0:T(8,128)(2,1)S(1)} %bitcast.288, f32[32,32,3072]{2,1,0:T(8,128)S(1)} %fusion.36), kind=kOutput, calls=%fused_computation.293 | convolution fusion | flops 4860936192 | bytes 23592960 | tf_op jit(solution)/shard_map/dot_general | solution.py:130
  126.7 14.9 %all_gather.3 = bf16[32,256,8]{0,2,1:T(8,128)(2,1)S(1)} all-gather(bf16[32,32,8]{0,2,1:T(8,128)(2,1)S(1)} %copy.45), channel_id=1, replica_groups=mesh['lat'=4,'lon'=8] {'lon'}, dimensions={1}, use_global_device_ids=true | all-gather | bytes 147456 | tf_op jit(solution)/shard_map/all_gather | solution.py:136
  142.9 57.9 %gather_fusion = bf16[16384,8]{1,0:T(8,128)(2,1)} fusion(bf16[8192,8]{1,0:T(8,128)(2,1)S(1)} %copy.47, s32[16384]{0:T(1024)S(1)} %copy-done.10), kind=kCustom, calls=%fused_computation | custom fusion | bytes 589824 | tf_op jit(solution)/shard_map/gather | solution.py:138
  200.8 4.7 %fusion.25 = f32[64,64,8]{2,1,0:T(8,128)S(1)} fusion(bf16[4,64,64,8]{3,2,1,0:T(8,128)(2,1)} %bitcast.180, f32[4,64,64]{2,1,0:T(8,128)S(1)} %copy-done.13), kind=kLoop, calls=%fused_computation.112 | loop fusion | flops 360448 | bytes 458752 | tf_op jit(solution)/shard_map/reduce_sum | solution.py:139
  205.5 5.1 %fusion.47 = (bf16[64,64,192]{2,1,0:T(8,128)(2,1)S(1)}, f32[64,64,192]{2,1,0:T(8,128)}) fusion(bf16[64,64,192]{2,1,0:T(8,128)(2,1)S(1)} %copy-done.8, f32[64,64]{1,0:T(8,128)S(1)} %copy-done.12, f32[64,64,8]{2,1,0:T(8,128)S(1)} %fusion.25, f32[8,192]{1,0:T(8,128)S(1)} %copy-done.19), kind=kOutput, calls=%fused_computation.145 | convolution fusion | flops 78643200 | bytes 6445056 | tf_op jit(solution)/shard_map/dot_general | solution.py:142
  242.0 73.9 %fusion.194 = (f32[64,64]{1,0:T(8,128)S(1)}, f32[64,64,192]{2,1,0:T(8,128)S(1)}) fusion(f32[192]{0:T(256)S(1)} %bitcast.233, bf16[3,70,192]{2,1,0:T(8,128)(2,1)S(1)} %get-tuple-element.13, bf16[64,70,192]{2,1,0:T(8,128)(2,1)} %slice.1213, f32[192]{0:T(256)S(1)} %bitcast.234, f32[192]{0:T(256)S(1)} %bitcast.235, f32[192]{0:T(256)S(1)} %bitcast.236, ...), kind=kLoop, calls=%fused_computation.350 | loop fusion | flops 214691840 | bytes 16091392 | tf_op jit(solution)/shard_map/reduce_sum | solution.py:44
  317.9 9.9 %fusion.207 = (bf16[64,64,192]{2,1,0:T(8,128)(2,1)S(1)}, f32[64,64,192]{2,1,0:T(8,128)}) fusion(bf16[2,768,192]{1,2,0:T(8,128)(2,1)S(1)} %copy-done.96, f32[64,64,192]{2,1,0:T(8,128)} %copy-done.3, f32[192]{0:T(256)S(1)} %bitcast.286, f32[64,64]{1,0:T(8,128)S(1)} %add_rsqrt_fusion.1, f32[64,64]{1,0:T(8,128)S(1)} %broadcast_multiply_fusion.1, ...), kind=kOutput, calls=%fused_computation.363 | convolution fusion | flops 2452094976 | bytes 15893504 | tf_op jit(solution)/shard_map/dot_general | solution.py:74
  360.6 76.5 %fusion.193 = (f32[64,64]{1,0:T(8,128)S(1)}, f32[64,64,192]{2,1,0:T(8,128)S(1)}) fusion(f32[192]{0:T(256)S(1)} %bitcast.186, bf16[3,70,192]{2,1,0:T(8,128)(2,1)S(1)} %get-tuple-element.11, bf16[64,70,192]{2,1,0:T(8,128)(2,1)} %slice.1302, f32[192]{0:T(256)S(1)} %bitcast.187, f32[192]{0:T(256)S(1)} %bitcast.244, f32[192]{0:T(256)S(1)} %bitcast.245, ...), kind=kLoop, calls=%fused_computation.349 | loop fusion | flops 214691840 | bytes 16091392 | tf_op jit(solution)/shard_map/reduce_sum | solution.py:44
  440.4 9.6 %fusion.210 = (bf16[64,64,192]{2,1,0:T(8,128)(2,1)}, f32[64,64,192]{2,1,0:T(8,128)}) fusion(f32[64,64,192]{2,1,0:T(8,128)} %get-tuple-element.133, bf16[2,768,192]{1,2,0:T(8,128)(2,1)S(1)} %copy-done.97, f32[64,64,192]{2,1,0:T(8,128)} %copy-done.2, f32[192]{0:T(256)S(1)} %bitcast.285, f32[64,64]{1,0:T(8,128)S(1)} %add_rsqrt_fusion, ...), kind=kOutput, calls=%fused_computation.364 | convolution fusion | flops 2449735680 | bytes 11699200 | tf_op jit(solution)/shard_map/dot_general | solution.py:74
  450.1 7.3 %fusion.215 = f32[1,64,64]{2,0,1:T(1,128)S(1)} fusion(f32[64,64,192]{2,1,0:T(8,128)} %get-tuple-element.135, f32[192,1,1]{0,1,2:T(1,128)S(1)} %bitcast.284), kind=kOutput, calls=%fused_computation.366 | convolution fusion | flops 9437184 | bytes 3162880 | tf_op jit(solution)/shard_map/dot_general | solution.py:169
  (290 shorter events, 96.3 us)
Async XLA Ops:
  0.6 105.3 %copy-start = (bf16[768,768]{1,0:T(8,128)(2,1)S(1)}, bf16[768,768]{1,0:T(8,128)(2,1)}, u32[]{:S(2)}) copy-start(bf16[768,768]{1,0:T(8,128)(2,1)} %param.25) | copy-start | bytes 3538948
  2.5 10.9 %copy-start.9 = (bf16[32,32,768]{2,1,0:T(8,128)(2,1)S(1)}, bf16[32,32,768]{2,1,0:T(8,128)(2,1)}, u32[]{:S(2)}) copy-start(bf16[32,32,768]{2,1,0:T(8,128)(2,1)} %param.19) | copy-start | bytes 4718596
  2.6 10.9 %copy-start.99 = (f32[768]{0:T(1024)S(1)}, f32[768]{0:T(1024)}, u32[]{:S(2)}) copy-start(f32[768]{0:T(1024)} %param.28) | copy-start | bytes 9220
  8.9 25.1 %collective-permute-start = (bf16[32,8,1536]{2,1,0:T(8,128)(2,1)}, bf16[32,8,1536]{2,1,0:T(8,128)(2,1)}, u32[]{:S(2)}, u32[]{:S(2)}) collective-permute-start(bf16[32,8,1536]{2,1,0:T(8,128)(2,1)} %get-tuple-element.8), channel_id=1, source_target_pairs={{0,1},{1,2},{2,3},{3,4},{4,5},{5,6},{6,7},{7,0},{8,9},{9,10},{10,1... | collective-permute-start | bytes 2359304 | tf_op jit(solution)/shard_map/ppermute | solution.py:21
  9.4 24.6 %collective-permute-start.1 = (bf16[32,8,1536]{2,1,0:T(8,128)(2,1)}, bf16[32,8,1536]{2,1,0:T(8,128)(2,1)}, u32[]{:S(2)}, u32[]{:S(2)}) collective-permute-start(bf16[32,8,1536]{2,1,0:T(8,128)(2,1)} %get-tuple-element.9), channel_id=1, source_target_pairs={{1,0},{2,1},{3,2},{4,3},{5,4},{6,5},{7,6},{0,7},{9,8},{10,9},{11,1... | collective-permute-start | bytes 2359304 | tf_op jit(solution)/shard_map/ppermute | solution.py:24
  125.4 17.5 %copy-start.10 = (s32[16384]{0:T(1024)S(1)}, s32[16384]{0:T(1024)}, u32[]{:S(2)}) copy-start(s32[16384]{0:T(1024)} %broadcast_clamp_fusion) | copy-start | bytes 196612
  142.9 57.9 %copy-start.13 = (f32[4,64,64]{2,1,0:T(8,128)S(1)}, f32[4,64,64]{2,1,0:T(8,128)}, u32[]{:S(2)}) copy-start(f32[4,64,64]{2,1,0:T(8,128)} %param.23) | copy-start | bytes 196612
  210.6 17.0 %copy-start.93 = (f32[2,192]{1,0:T(2,128)S(1)}, f32[2,192]{1,0:T(2,128)}, u32[]{:S(2)}) copy-start(f32[2,192]{1,0:T(2,128)} %param.34) | copy-start | bytes 4612
  210.6 6.7 %collective-permute-start.2 = (bf16[3,64,192]{2,1,0:T(8,128)(2,1)S(1)}, bf16[3,64,192]{2,1,0:T(8,128)(2,1)S(1)}, u32[]{:S(2)}, u32[]{:S(2)}) collective-permute-start(bf16[3,64,192]{2,1,0:T(8,128)(2,1)S(1)} %get-tuple-element.24), channel_id=1, source_target_pairs={{0,8},{8,16},{16,24},{24,0},{1,9},{9,17},{17,25},{25,1},{2,10},{10... | collective-permute-start | bytes 221192 | tf_op jit(solution)/shard_map/ppermute | solution.py:21
  212.7 6.6 %collective-permute-start.3 = (bf16[3,64,192]{2,1,0:T(8,128)(2,1)S(1)}, bf16[3,64,192]{2,1,0:T(8,128)(2,1)S(1)}, u32[]{:S(2)}, u32[]{:S(2)}) collective-permute-start(bf16[3,64,192]{2,1,0:T(8,128)(2,1)S(1)} %get-tuple-element.25), channel_id=1, source_target_pairs={{8,0},{16,8},{24,16},{0,24},{9,1},{17,9},{25,17},{1,25},{10,2},{18... | collective-permute-start | bytes 221192 | tf_op jit(solution)/shard_map/ppermute | solution.py:24
  219.4 7.5 %collective-permute-start.4 = (bf16[70,3,192]{2,1,0:T(4,128)(2,1)S(1)}, bf16[70,3,192]{2,1,0:T(4,128)(2,1)S(1)}, u32[]{:S(2)}, u32[]{:S(2)}) collective-permute-start(bf16[70,3,192]{2,1,0:T(4,128)(2,1)S(1)} %get-tuple-element.20), channel_id=1, source_target_pairs={{0,1},{1,2},{2,3},{3,4},{4,5},{5,6},{6,7},{7,0},{8,9},{9,10},{10,1... | collective-permute-start | bytes 241928 | tf_op jit(solution)/shard_map/ppermute | solution.py:21
  219.5 7.5 %collective-permute-start.5 = (bf16[70,3,192]{2,1,0:T(4,128)(2,1)S(1)}, bf16[70,3,192]{2,1,0:T(4,128)(2,1)S(1)}, u32[]{:S(2)}, u32[]{:S(2)}) collective-permute-start(bf16[70,3,192]{2,1,0:T(4,128)(2,1)S(1)} %get-tuple-element.21), channel_id=1, source_target_pairs={{1,0},{2,1},{3,2},{4,3},{5,4},{6,5},{7,6},{0,7},{9,8},{10,9},{11,1... | collective-permute-start | bytes 241928 | tf_op jit(solution)/shard_map/ppermute | solution.py:24
  227.5 1.4 collective-permute-start.6
  228.9 5.1 %collective-permute-start.7 = (bf16[3,70,192]{2,1,0:T(8,128)(2,1)S(1)}, bf16[3,70,192]{2,1,0:T(8,128)(2,1)S(1)}, u32[]{:S(2)}, u32[]{:S(2)}) collective-permute-start(bf16[3,70,192]{2,1,0:T(8,128)(2,1)S(1)} %collective-permute-done.6), channel_id=1, source_target_pairs={{0,2},{2,0},{1,3},{3,1},{4,6},{6,4},{5,7},{7,5},{8,10},{10,8},{9,1... | collective-permute-start | bytes 241928 | tf_op jit(solution)/shard_map/ppermute | solution.py:36
  234.0 7.5 %collective-permute-start.8 = (bf16[3,70,192]{2,1,0:T(8,128)(2,1)S(1)}, bf16[3,70,192]{2,1,0:T(8,128)(2,1)S(1)}, u32[]{:S(2)}, u32[]{:S(2)}) collective-permute-start(bf16[3,70,192]{2,1,0:T(8,128)(2,1)S(1)} %collective-permute-done.7), channel_id=1, source_target_pairs={{0,4},{4,0},{1,5},{5,1},{2,6},{6,2},{3,7},{7,3},{8,12},{12,8},{9,1... | collective-permute-start | bytes 241928 | tf_op jit(solution)/shard_map/ppermute | solution.py:36
  327.8 16.9 %copy-start.15 = (s32[64,64]{1,0:T(8,128)S(1)}, s32[64,64]{1,0:T(8,128)}, u32[]{:S(2)}) copy-start(s32[64,64]{1,0:T(8,128)} %param.21) | copy-start | bytes 49156
  327.9 4.8 %collective-permute-start.10 = (bf16[3,64,192]{2,1,0:T(8,128)(2,1)S(1)}, bf16[3,64,192]{2,1,0:T(8,128)(2,1)S(1)}, u32[]{:S(2)}, u32[]{:S(2)}) collective-permute-start(bf16[3,64,192]{2,1,0:T(8,128)(2,1)S(1)} %get-tuple-element.23), channel_id=1, source_target_pairs={{8,0},{16,8},{24,16},{0,24},{9,1},{17,9},{25,17},{1,25},{10,2},{18... | collective-permute-start | bytes 221192 | tf_op jit(solution)/shard_map/ppermute | solution.py:24
  329.4 5.5 %collective-permute-start.9 = (bf16[3,64,192]{2,1,0:T(8,128)(2,1)S(1)}, bf16[3,64,192]{2,1,0:T(8,128)(2,1)S(1)}, u32[]{:S(2)}, u32[]{:S(2)}) collective-permute-start(bf16[3,64,192]{2,1,0:T(8,128)(2,1)S(1)} %get-tuple-element.22), channel_id=1, source_target_pairs={{0,8},{8,16},{16,24},{24,0},{1,9},{9,17},{17,25},{25,1},{2,10},{10... | collective-permute-start | bytes 221192 | tf_op jit(solution)/shard_map/ppermute | solution.py:21
  335.0 6.6 %collective-permute-start.11 = (bf16[70,3,192]{2,1,0:T(4,128)(2,1)S(1)}, bf16[70,3,192]{2,1,0:T(4,128)(2,1)S(1)}, u32[]{:S(2)}, u32[]{:S(2)}) collective-permute-start(bf16[70,3,192]{2,1,0:T(4,128)(2,1)S(1)} %get-tuple-element.16), channel_id=1, source_target_pairs={{0,1},{1,2},{2,3},{3,4},{4,5},{5,6},{6,7},{7,0},{8,9},{9,10},{10,1... | collective-permute-start | bytes 241928 | tf_op jit(solution)/shard_map/ppermute | solution.py:21
  335.1 6.5 %collective-permute-start.12 = (bf16[70,3,192]{2,1,0:T(4,128)(2,1)S(1)}, bf16[70,3,192]{2,1,0:T(4,128)(2,1)S(1)}, u32[]{:S(2)}, u32[]{:S(2)}) collective-permute-start(bf16[70,3,192]{2,1,0:T(4,128)(2,1)S(1)} %get-tuple-element.17), channel_id=1, source_target_pairs={{1,0},{2,1},{3,2},{4,3},{5,4},{6,5},{7,6},{0,7},{9,8},{10,9},{11,1... | collective-permute-start | bytes 241928 | tf_op jit(solution)/shard_map/ppermute | solution.py:24
  344.0 2.4 collective-permute-start.13
  346.4 5.7 %collective-permute-start.14 = (bf16[3,70,192]{2,1,0:T(8,128)(2,1)}, bf16[3,70,192]{2,1,0:T(8,128)(2,1)S(1)}, u32[]{:S(2)}, u32[]{:S(2)}) collective-permute-start(bf16[3,70,192]{2,1,0:T(8,128)(2,1)} %collective-permute-done.13), channel_id=1, source_target_pairs={{0,2},{2,0},{1,3},{3,1},{4,6},{6,4},{5,7},{7,5},{8,10},{10,8},{9,1... | collective-permute-start | bytes 241928 | tf_op jit(solution)/shard_map/ppermute | solution.py:36
  352.2 7.9 %collective-permute-start.15 = (bf16[3,70,192]{2,1,0:T(8,128)(2,1)S(1)}, bf16[3,70,192]{2,1,0:T(8,128)(2,1)S(1)}, u32[]{:S(2)}, u32[]{:S(2)}) collective-permute-start(bf16[3,70,192]{2,1,0:T(8,128)(2,1)S(1)} %collective-permute-done.14), channel_id=1, source_target_pairs={{0,4},{4,0},{1,5},{5,1},{2,6},{6,2},{3,7},{7,3},{8,12},{12,8},{9,1... | collective-permute-start | bytes 241928 | tf_op jit(solution)/shard_map/ppermute | solution.py:36
  450.1 12.0 %copy-start.1 = (bf16[768,768]{1,0:T(8,128)(2,1)S(1)}, bf16[768,768]{1,0:T(8,128)(2,1)}, u32[]{:S(2)}) copy-start(bf16[768,768]{1,0:T(8,128)(2,1)} %param.25) | copy-start | bytes 3538948
  (95 other events, 462.0 us)
where the time goes:
time: 466 us; the launch traced here: 462 us
  other arithmetic  176 us (38%)
  local copies, waits for them, and re-layouts  143 us (31%)
  matrix products  76.8 us (16%)
  waiting for transfers between devices  28.3 us (6%)
  starting transfers between devices  20.5 us (4%)
  blocking collectives  14.9 us (3%)
    reduce_sum x2, other arithmetic, layer_scale(): center = values - jnp.mean(values, axis=-1, keepdims=True)  150 us
    gather x1, local copies, waits for them, and re-layouts, body(): picked = band_flat[overlay_cell_index].astype(jnp.float32)  57.9 us
    reshape x3, local copies, waits for them, and re-layouts, to_windows(): tensor.reshape(row_total // WR, WR, column_total // WC, WC, HEADS, HD)  20.4 us
    dot_general x2, matrix products, ocean_mlp(): return jnp.dot(active, down_weight, preferred_element_type=jnp.float32)  19.5 us
    transpose x3, local copies, waits for them, and re-layouts, to_windows(): return shaped.transpose(0, 2, 4, 1, 3, 5).reshape(-1, HEADS, WR * WC, HD)  19 us
    all_gather x1, blocking collectives, body(): band_flux = lax.all_gather(fluxes, 'lon', axis=1, tiled=True)  14.9 us
    ppermute x5, starting transfers between devices, with_halo(): lax.ppermute(lax.slice_in_dim(block, 0, width, axis=dim), axis, backward)  13.6 us
    ppermute x6, waiting for transfers between devices, swapped(): return lax.ppermute(block, axis, route)  12.2 us
  transfers between devices with their start and end apart: 16, of which 11 were waited for; matrix products, arithmetic and copies ran while one was open for 8% of the time, Pallas kernels for 0%

commit v1 on v0

v1 whole, which is shorter than its diff:
```python
import functools

import jax
import jax.numpy as jnp
from jax import lax
from jax.experimental import pallas as pl
from jax.experimental.pallas import tpu as pltpu
from jax.sharding import PartitionSpec as P

HEADS = 12
HD = 64
WR = 8
WC = 16
EPS = 1e-06
LANES = 128
SUB = 8
HALO = 8
REACH = 3
F32 = jnp.float32
BF16 = jnp.bfloat16

VMEM = pl.BlockSpec(memory_space=pltpu.VMEM)
SMEM = pl.BlockSpec(memory_space=pltpu.SMEM)
HBM = pl.BlockSpec(memory_space=pl.ANY)


def gelu(x):
    inner = x * (0.7978845608028654 + 0.035677408136300125 * (x * x))
    half = 0.5 * x
    return half + half * jnp.tanh(inner)


def ring(count, step):
    return [(i, (i + step) % count) for i in range(count)]


def atmosphere_kernel(
    is_edge, x_ref, halo_ref, gains_ref, wqkv_hbm, wout_hbm, wup_hbm, wdown_hbm, wflux_ref,
    second_ref, flux_ref,
    x_s, normed_s, qkv_s, att_s, first_s, act_s, wqkv, wout, wup, wdown, sems,
):
    half = WC // 2
    copies = [
        pltpu.make_async_copy(wqkv_hbm, wqkv, sems.at[0]),
        pltpu.make_async_copy(wout_hbm, wout, sems.at[1]),
        pltpu.make_async_copy(wup_hbm, wup, sems.at[2]),
        pltpu.make_async_copy(wdown_hbm, wdown, sems.at[3]),
    ]
    for copy in copies:
        copy.start()
    rows = x_ref.shape[0]
    cols = x_ref.shape[1]
    width = x_ref.shape[2]
    cells = WR * WC
    blocks = rows // WR
    for m in range(blocks):
        own = x_ref[m * WR : (m + 1) * WR].astype(F32)
        if is_edge:
            halo = halo_ref[m * WR : (m + 1) * WR].astype(F32)
            window = jnp.concatenate([own[:, cols - half :], halo], axis=1)
        else:
            window = own[:, half : half + WC]
        flat = window.reshape(cells, width)
        x_s[m * cells : (m + 1) * cells] = flat
        scale = lax.rsqrt(jnp.mean(flat * flat, axis=-1, keepdims=True) + EPS)
        normed_s[m * cells : (m + 1) * cells] = (flat * scale * gains_ref[0:1]).astype(BF16)
    copies[0].wait()
    step = 256
    for n in range(0, wqkv.shape[1], step):
        qkv_s[:, n : n + step] = jnp.dot(
            normed_s[...], wqkv[:, n : n + step], preferred_element_type=F32
        ).astype(BF16)
    lane = lax.broadcasted_iota(jnp.int32, (cells, LANES), 1)
    low = lane < HD
    ones_low = jnp.where(low, 1.0, 0.0).astype(BF16)
    ones_high = jnp.where(low, 0.0, 1.0).astype(BF16)
    norm = HD ** (-0.5)
    mask_low = jnp.where(low, norm, 0.0).astype(BF16)
    mask_high = jnp.where(low, 0.0, norm).astype(BF16)
    for m in range(blocks):
        span = pl.ds(m * cells, cells)
        for pair in range(HEADS // 2):
            base = pair * LANES
            q = qkv_s[span, base : base + LANES]
            k = qkv_s[span, width + base : width + base + LANES]
            v = qkv_s[span, 2 * width + base : 2 * width + base + LANES]
            k2 = jnp.concatenate([k * mask_low, k * mask_high], axis=0)
            scores = lax.dot_general(
                q, k2, (((1,), (1,)), ((), ())), preferred_element_type=F32
            )
            probs = []
            for head in range(2):
                s = scores[:, head * cells : (head + 1) * cells]
                probs.append(jnp.exp(s - jnp.max(s, axis=-1, keepdims=True)).astype(BF16))
            both = jnp.concatenate(probs, axis=1)
            v2 = jnp.concatenate(
                [
                    jnp.concatenate([v * ones_low, ones_low], axis=1),
                    jnp.concatenate([v * ones_high, ones_high], axis=1),
                ],
                axis=0,
            )
            mixed = jnp.dot(both, v2, preferred_element_type=F32)
            att_s[span, base : base + LANES] = (
                mixed[:, :LANES] / mixed[:, LANES:]
            ).astype(BF16)
    copies[1].wait()
    for n in range(0, width, step):
        first_s[:, n : n + step] = x_s[:, n : n + step] + jnp.dot(
            att_s[...], wout[:, n : n + step], preferred_element_type=F32
        )
    for m in range(blocks):
        flat = first_s[m * cells : (m + 1) * cells]
        scale = lax.rsqrt(jnp.mean(flat * flat, axis=-1, keepdims=True) + EPS)
        normed_s[m * cells : (m + 1) * cells] = (flat * scale * gains_ref[1:2]).astype(BF16)
    copies[2].wait()
    for n in range(0, wup.shape[1], step):
        act_s[:, n : n + step] = gelu(
            jnp.dot(normed_s[...], wup[:, n : n + step], preferred_element_type=F32)
        ).astype(BF16)
    copies[3].wait()
    flux = None
    for n in range(0, width, step):
        second = first_s[:, n : n + step] + jnp.dot(
            act_s[...], wdown[:, n : n + step], preferred_element_type=F32
        )
        second_ref[:, n : n + step] = second
        part = lax.dot_general(
            wflux_ref[:, n : n + step],
            second.astype(BF16),
            (((1,), (1,)), ((), ())),
            preferred_element_type=F32,
        )
        flux = part if flux is None else flux + part
    for g in range(flux_ref.shape[0]):
        flux_ref[g] = flux[:, g * 256 : (g + 1) * 256].astype(BF16)


def atmosphere(is_edge, x, halo, gains, wqkv, wout, wup, wdown, wflux_t):
    rows, cols, width = x.shape
    total = rows * WC
    ffn = wup.shape[1]
    channels = wflux_t.shape[0]
    return pl.pallas_call(
        functools.partial(atmosphere_kernel, is_edge),
        out_shape=(
            jax.ShapeDtypeStruct((total, width), F32),
            jax.ShapeDtypeStruct((total // 256, channels, 256), BF16),
        ),
        in_specs=[VMEM, VMEM, VMEM, HBM, HBM, HBM, HBM, VMEM],
        out_specs=(VMEM, VMEM),
        scratch_shapes=[
            pltpu.VMEM((total, width), F32),
            pltpu.VMEM((total, width), BF16),
            pltpu.VMEM((total, 3 * width), BF16),
            pltpu.VMEM((total, width), BF16),
            pltpu.VMEM((total, width), F32),
            pltpu.VMEM((total, ffn), BF16),
            pltpu.VMEM(wqkv.shape, BF16),
            pltpu.VMEM(wout.shape, BF16),
            pltpu.VMEM(wup.shape, BF16),
            pltpu.VMEM(wdown.shape, BF16),
            pltpu.SemaphoreType.DMA((4,)),
        ],
        name="atm_edge" if is_edge else "atm_own",
    )(x, halo, gains, wqkv, wout, wup, wdown, wflux_t)


def regrid_kernel(band_cols, own_cols, table_ref, meta_ref, out_ref):
    groups = table_ref.shape[0]
    channels = table_ref.shape[1]
    depth = table_ref.shape[2]
    table = (
        table_ref[...].astype(F32).reshape(groups * channels, depth).astype(BF16)
    )
    entries = (meta_ref.shape[0] - 1) // 2
    total = meta_ref.shape[1]
    step = 640
    halves = own_cols // WC
    per_half = groups // (band_cols // own_cols * halves)
    bits = groups.bit_length() - 1

    def chunk(i, carry):
        span = pl.ds(pl.multiple_of(i * step, LANES), step)
        place = meta_ref[0:entries, span].astype(jnp.int32)
        row = place // band_cols
        col = place % band_cols
        col = jnp.where(col < WC // 2, col + band_cols, col) - WC // 2
        part = (col // WC) * per_half + row // (WR * 2)
        slot = (row % (WR * 2)) * WC + col % WC
        slot_f = slot.astype(F32)
        total_flux = None
        iota = lax.broadcasted_iota(jnp.int32, (depth, step), 0).astype(F32)
        for e in range(entries):
            hot = jnp.where(iota == slot_f[e : e + 1], 1.0, 0.0).astype(BF16)
            picked = jnp.dot(table, hot, preferred_element_type=F32)
            level = [picked[g * channels : (g + 1) * channels] for g in range(groups)]
            code = jnp.broadcast_to(part[e : e + 1], (channels, step))
            for bit in range(bits):
                odd = ((code >> bit) & 1) == 1
                level = [
                    jnp.where(odd, level[2 * g + 1], level[2 * g])
                    for g in range(len(level) // 2)
                ]
            term = level[0] * meta_ref[entries + e : entries + e + 1, span]
            total_flux = term if total_flux is None else total_flux + term
        wet = meta_ref[2 * entries : 2 * entries + 1, span]
        out_ref[0:channels, span] = total_flux * wet
        out_ref[channels : 2 * channels, span] = jnp.broadcast_to(wet, (channels, step))
        return carry

    lax.fori_loop(0, total // step, chunk, 0)


def regrid(table, meta, band_cols, own_cols):
    channels = table.shape[1]
    return pl.pallas_call(
        functools.partial(regrid_kernel, band_cols, own_cols),
        out_shape=jax.ShapeDtypeStruct((2 * channels, meta.shape[1]), F32),
        in_specs=[VMEM, VMEM],
        out_specs=VMEM,
        name="regrid",
    )(table, meta)


def ocean_kernel(
    flags_ref, own_ref, west_ref, east_ref, south_ref, north_ref, fold_ref,
    flux_ref, flux_south_ref, flux_north_ref, lift_ref, flip_ref,
    taps_ref, gains_ref, up_ref, down_ref, head_ref,
    out_ref, sst_ref,
    field_a, field_b, wet_s, planes_s, normed_s,
):
    rows, cols, channels = own_ref.shape
    wide = cols + 2 * HALO
    fluxes = flux_ref.shape[0] // 2
    upper = channels - LANES
    bottom = flags_ref[0]
    top = flags_ref[1]
    run = SUB * wide

    def assemble(flux, ocean, at):
        force = flux[0:fluxes]
        high = force.astype(BF16)
        lowp = (force - high.astype(F32)).astype(BF16)
        lhs = jnp.concatenate(
            [high.astype(F32), lowp.astype(F32), high.astype(F32), flux[fluxes:]], axis=0
        ).astype(BF16)
        lifted = lax.dot_general(
            lhs, lift_ref[...], (((0,), (0,)), ((), ())), preferred_element_type=F32
        )
        wet = lifted[:, 2 * LANES :]
        span = pl.ds(at, SUB)
        wet_s[span] = wet.reshape(SUB, wide, LANES)
        field_a[0, span] = (lifted[:, :LANES] + wet * ocean[:, :LANES]).reshape(
            SUB, wide, LANES
        )
        rest = jnp.concatenate(
            [ocean[:, LANES:], jnp.zeros((run, 2 * LANES - channels), F32)], axis=1
        )
        field_a[1, span] = (lifted[:, LANES : 2 * LANES] + wet * rest).reshape(
            SUB, wide, LANES
        )

    south = south_ref[...].astype(F32).reshape(run, channels)
    assemble(flux_south_ref[...] * bottom, south, 0)
    def middle(g, carry):
        own_rows = pl.ds(pl.multiple_of(g * SUB, SUB), SUB)
        ocean = jnp.concatenate(
            [
                west_ref[own_rows].astype(F32),
                own_ref[own_rows].astype(F32),
                east_ref[own_rows].astype(F32),
            ],
            axis=1,
        ).reshape(run, channels)
        lanes = pl.ds(pl.multiple_of(g * run, LANES), run)
        assemble(flux_ref[:, lanes], ocean, pl.multiple_of(HALO + g * SUB, SUB))
        return carry
    lax.fori_loop(0, rows // SUB, middle, 0)
    folded = [
        jnp.dot(flip_ref[...], fold_ref[SUB - 1 - k], preferred_element_type=F32)
        for k in range(SUB)
    ]
    folded = jnp.concatenate(folded, axis=0)
    north = north_ref[...].astype(F32).reshape(run, channels)
    north = jnp.where(top > 0.5, folded, north)
    flux_north = jnp.where(
        top > 0.5, flux_ref[:, rows * wide :], flux_north_ref[...]
    )
    assemble(flux_north, north, HALO + rows)

    lane = lax.broadcasted_iota(jnp.int32, (2 * SUB, LANES), 1)

    def block(index, src, dst, row0, row1, count, per_body, planes, col0):
        reach = planes + 2 * REACH

        def build(i, carry):
            for t in range(2):
                for p in range(reach):
                    at = pl.ds(col0 - REACH + p, SUB, stride=planes)
                    a = src[t, row0 - REACH + i, at, :]
                    b = src[t, row1 - REACH + i, at, :]
                    planes_s[t, i, p] = jnp.concatenate([a, b], axis=0).astype(BF16)
            return carry

        lax.fori_loop(0, count + 2 * REACH, build, 0)
        cells = planes * 2 * SUB

        def convolve(i, slot, at):
            variant = jnp.where(row1 + i >= HALO + rows, 1, 0)
            sums = [[None] * planes for _ in range(2)]
            for t in range(2):
                for p0 in range(0, planes, 4):
                    group = range(p0, min(p0 + 4, planes))
                    acc = {}
                    for a in range(7):
                        xs = {
                            p: planes_s[t, i + a, p].astype(F32)
                            for p in range(p0, group[-1] + 7)
                        }
                        for b in range(7):
                            w = taps_ref[index, variant, t, 7 * a + b].astype(F32)
                            for p in group:
                                term = xs[p + b] * w
                                acc[p] = acc[p] + term if p in acc else term
                    for p in group:
                        sums[t][p] = acc[p]
            for p in range(planes):
                lo, hi = sums[0][p], sums[1][p]
                mean = jnp.sum(lo + hi, axis=-1, keepdims=True) * (1.0 / channels)
                lo = lo - mean
                hi = jnp.where(lane < upper, hi - mean, 0.0)
                var = jnp.sum(lo * lo + hi * hi, axis=-1, keepdims=True) * (1.0 / channels)
                scale = lax.rsqrt(var + EPS)
                normed_s[slot, at + p * 2 * SUB : at + (p + 1) * 2 * SUB, :LANES] = (
                    lo * scale * gains_ref[index, 0:1]
                ).astype(BF16)
                normed_s[slot, at + p * 2 * SUB : at + (p + 1) * 2 * SUB, LANES:] = (
                    hi * scale * gains_ref[index, 1:2]
                ).astype(BF16)

        def mlp(i, slot):
            normed = normed_s[slot, 0 : per_body * cells]
            active = gelu(
                jnp.dot(normed, up_ref[index], preferred_element_type=F32)
            ).astype(BF16)
            delta = jnp.dot(active, down_ref[index], preferred_element_type=F32)
            for j in range(per_body):
                for p in range(planes):
                    for h, base in enumerate((row0, row1)):
                        at = pl.ds(col0 + p, SUB, stride=planes)
                        line = base + i + j
                        wet = wet_s[line, at, :]
                        first = j * cells + p * 2 * SUB + h * SUB
                        for t in range(2):
                            dst[t, line, at, :] = src[t, line, at, :] + wet * delta[
                                first : first + SUB, t * LANES : (t + 1) * LANES
                            ]

        def body(g, carry):
            i = g * per_body
            for j in range(per_body):
                convolve(i + j, 0, j * cells)
            mlp(i, 0)
            return carry

        lax.fori_loop(0, count // per_body, body, 0)

    half0 = (rows + 2 * REACH) // 2
    block(0, field_a, field_b, HALO - REACH, HALO - REACH + half0, half0, 5, 9, HALO - 4)
    block(1, field_b, field_a, HALO, HALO + rows // 2, rows // 2, 4, cols // SUB, HALO)

    def finish(i, carry):
        pooled = [None, None]
        count = None
        for a in range(2):
            line = HALO + 2 * i + a
            lo = field_a[0, line, pl.ds(HALO, cols), :]
            hi = field_a[1, line, pl.ds(HALO, cols), :]
            out_ref[2 * i + a] = jnp.concatenate([lo, hi[:, :upper]], axis=1).astype(BF16)
            for b in range(2):
                at = pl.ds(HALO + b, cols // 2, stride=2)
                for t in range(2):
                    value = field_a[t, line, at, :]
                    pooled[t] = value if pooled[t] is None else pooled[t] + value
                wet = wet_s[line, at, :]
                count = wet if count is None else count + wet
        dot = jnp.sum(
            pooled[0] * head_ref[0:1] + pooled[1] * head_ref[1:2], axis=-1, keepdims=True
        )
        sst_ref[i] = dot / jnp.maximum(count, 1.0)
        return carry

    lax.fori_loop(0, rows // 2, finish, 0)


def ocean(flags, pieces, flux, flux_south, flux_north, lift, flip, taps, gains, up, down, head):
    own = pieces[0]
    rows, cols, channels = own.shape
    tall = rows + 2 * HALO
    wide = cols + 2 * HALO
    return pl.pallas_call(
        ocean_kernel,
        out_shape=(
            jax.ShapeDtypeStruct((rows, cols, channels), BF16),
            jax.ShapeDtypeStruct((rows // 2, cols // 2, LANES), F32),
        ),
        in_specs=[SMEM] + [VMEM] * 16,
        out_specs=(VMEM, VMEM),
        scratch_shapes=[
            pltpu.VMEM((2, tall, wide, LANES), F32),
            pltpu.VMEM((2, tall, wide, LANES), F32),
            pltpu.VMEM((tall, wide, LANES), F32),
            pltpu.VMEM((2, rows // 2 + REACH + 2 * REACH, 15, 2 * SUB, LANES), BF16),
            pltpu.VMEM((2, 720, 2 * LANES), BF16),
        ],
        name="ocean",
    )(flags, *pieces, flux, flux_south, flux_north, lift, flip, taps, gains, up, down, head)


def update_kernel(own_ref, edge_ref, back_ref, sst_ref, embed_ref, out_ref):
    half = WC // 2
    width = own_ref.shape[1]
    cols = sst_ref.shape[1]
    own = own_ref[...].reshape(WR, WC, width)
    edge = edge_ref[...].reshape(WR, WC, width)
    back = back_ref[...].astype(F32)
    second = jnp.concatenate([back, own, edge[:, :half]], axis=1)
    sst = sst_ref[...][:, :, 0:1]
    out_ref[...] = (
        second + sst * embed_ref[...].reshape(1, 1, width)
    ).astype(BF16)


def update(own, edge, back, sst, embed, rows, cols):
    width = own.shape[1]
    cells = WR * WC
    half = WC // 2
    return pl.pallas_call(
        update_kernel,
        grid=(rows // WR,),
        out_shape=jax.ShapeDtypeStruct((rows, cols, width), BF16),
        in_specs=[
            pl.BlockSpec((cells, width), lambda m: (m, 0)),
            pl.BlockSpec((cells, width), lambda m: (m, 0)),
            pl.BlockSpec((WR, half, width), lambda m: (m, 0, 0)),
            pl.BlockSpec((WR, cols, LANES), lambda m: (m, 0, 0)),
            pl.BlockSpec((1, width), lambda m: (0, 0)),
        ],
        out_specs=pl.BlockSpec((WR, cols, width), lambda m: (m, 0, 0)),
        name="update",
    )(own, edge, back, sst, embed)


def body(
    atmos_features,
    ocean_features,
    wet_cell_mask,
    overlay_cell_index,
    remap_weight,
    query_key_value_weight,
    attention_out_weight,
    feedforward_up_weight,
    feedforward_down_weight,
    attention_gain,
    feedforward_gain,
    flux_head_weight,
    surface_temp_embedding,
    forcing_lift_weight,
    depthwise_kernels,
    ocean_norm_gains,
    ocean_up_weights,
    ocean_down_weights,
    surface_temp_head,
):
    arows, acols, width = atmos_features.shape
    rows, cols, channels = ocean_features.shape
    entries = overlay_cell_index.shape[0]
    half = WC // 2
    lat_index = lax.axis_index("lat")
    lat_count = lax.axis_size("lat")
    lon_count = lax.axis_size("lon")
    right, left = ring(lon_count, 1), ring(lon_count, -1)
    up_lat, down_lat = ring(lat_count, 1), ring(lat_count, -1)
    mirror = [(i, lon_count - 1 - i) for i in range(lon_count)]
    wide = cols + 2 * HALO
    run = SUB * wide
    is_top = lat_index == lat_count - 1

    x_halo = lax.ppermute(atmos_features[:, :half], "lon", left)
    west = lax.ppermute(ocean_features[:, cols - HALO :], "lon", right)
    east = lax.ppermute(ocean_features[:, :HALO], "lon", left)
    meta = jnp.concatenate(
        [
            overlay_cell_index.astype(F32),
            remap_weight,
            wet_cell_mask.astype(F32)[None],
        ],
        axis=0,
    )
    meta_west = lax.ppermute(meta[:, :, cols - HALO :], "lon", right)
    meta_east = lax.ppermute(meta[:, :, :HALO], "lon", left)

    gains = jnp.stack([attention_gain, feedforward_gain])
    wflux_t = flux_head_weight.T
    weights = (
        gains,
        query_key_value_weight,
        attention_out_weight,
        feedforward_up_weight,
        feedforward_down_weight,
        wflux_t,
    )
    second_own, flux_own = atmosphere(False, atmos_features, atmos_features[:, :half], *weights)

    south_strip = jnp.concatenate([west[:SUB], ocean_features[:SUB], east[:SUB]], axis=1)
    north_strip = jnp.concatenate(
        [west[rows - SUB :], ocean_features[rows - SUB :], east[rows - SUB :]], axis=1
    )
    north = lax.ppermute(south_strip, "lat", down_lat)
    south = lax.ppermute(north_strip, "lat", up_lat)
    fold = lax.ppermute(north_strip, "lon", mirror)
    meta_wide = jnp.concatenate([meta_west, meta, meta_east], axis=2).reshape(
        meta.shape[0], rows * wide
    )
    meta_fold = lax.ppermute(meta_wide[:, (rows - SUB) * wide :], "lon", mirror)[:, ::-1]
    meta_all = jnp.concatenate([meta_wide, meta_fold], axis=1)

    second_edge, flux_edge = atmosphere(True, atmos_features, x_halo, *weights)
    fluxes = jnp.concatenate([flux_own, flux_edge], axis=0)
    table = lax.all_to_all(
        jnp.broadcast_to(fluxes, (lon_count,) + fluxes.shape), "lon", 0, 0
    )
    table = table.reshape((-1,) + fluxes.shape[1:])
    back = lax.ppermute(
        second_edge.reshape(arows, WC, width)[:, half:].astype(BF16), "lon", right
    )

    flux = regrid(table, meta_all, acols * lon_count, acols)
    flux_north = lax.ppermute(flux[:, :run], "lat", down_lat)
    flux_south = lax.ppermute(
        flux[:, (rows - SUB) * wide : rows * wide], "lat", up_lat
    )

    flags = jnp.stack([lat_index != 0, is_top]).astype(F32)
    lift_high = forcing_lift_weight.astype(BF16)
    lift_low = (forcing_lift_weight - lift_high.astype(F32)).astype(BF16)
    nf = forcing_lift_weight.shape[0]
    wet_row = (jnp.arange(nf) == 0).astype(BF16)[:, None] * jnp.ones((1, LANES), BF16)
    pad = 2 * LANES - channels
    zeros = jnp.zeros((nf, pad), BF16)
    lift = jnp.concatenate(
        [
            jnp.concatenate([part, zeros, jnp.zeros((nf, LANES), BF16)], axis=1)
            for part in (lift_high, lift_high, lift_low)
        ]
        + [jnp.concatenate([jnp.zeros((nf, 2 * LANES), BF16), wet_row], axis=1)],
        axis=0,
    )
    flip = (jnp.arange(wide)[:, None] + jnp.arange(wide)[None] == wide - 1).astype(BF16)
    blocks = depthwise_kernels.shape[0]
    taps = jnp.pad(depthwise_kernels.astype(BF16), ((0, 0), (0, 0), (0, pad)))
    taps = taps.reshape(blocks, 49, 2, LANES).transpose(0, 2, 1, 3)
    turned = jnp.where(is_top, taps[:, :, ::-1], taps)
    normal = jnp.broadcast_to(taps[:, :, :, None], (blocks, 2, 49, SUB, LANES))
    turned = jnp.broadcast_to(turned[:, :, :, None], (blocks, 2, 49, SUB, LANES))
    taps = jnp.stack(
        [
            jnp.concatenate([normal, normal], axis=3),
            jnp.concatenate([normal, turned], axis=3),
        ],
        axis=1,
    )
    ocean_gains = jnp.pad(ocean_norm_gains, ((0, 0), (0, pad))).reshape(blocks, 2, LANES)
    up = jnp.pad(ocean_up_weights, ((0, 0), (0, pad), (0, 0)))
    down = jnp.pad(ocean_down_weights, ((0, 0), (0, 0), (0, pad)))
    head = jnp.pad(surface_temp_head, (0, pad)).reshape(2, LANES)

    ocean_out, sst = ocean(
        flags,
        (ocean_features, west, east, south, north, fold),
        flux,
        flux_south,
        flux_north,
        lift,
        flip,
        taps,
        ocean_gains,
        up,
        down,
        head,
    )
    atmos_updated = update(
        second_own, second_edge, back, sst, surface_temp_embedding[None], arows, acols
    )
    return (atmos_updated, ocean_out)


def solution(mesh):
    plane = P("lat", "lon", None)
    stack = P(None, "lat", "lon")
    in_specs = (plane, plane, P("lat", "lon"), stack, stack) + (P(),) * 14
    return jax.shard_map(
        body, mesh=mesh, in_specs=in_specs, out_specs=(plane, plane), check_vma=False
    )
```

time: 466 us -> 144 us (0.31)
  other arithmetic: 176 us -> 10.1 us
  local copies, waits for them, and re-layouts: 143 us -> 11.7 us
  Pallas kernels: 0 us -> 86.7 us
  matrix products: 76.8 us -> 0 us
  waiting for transfers between devices: 28.3 us -> 0.03 us
  blocking collectives: 14.9 us -> 0 us
  starting transfers between devices: 20.5 us -> 33.5 us
    reduce_sum x8 -> x0, other arithmetic: 160 us -> none  [the longest x2 150 us: layer_scale(): center = values - jnp.mean(values, axis=-1, keepdims=True)]
    pallas_call x0 -> x5, Pallas kernels: none -> 86.7 us  [the longest x1 39.7 us: ocean(): pl.pallas_call(ocean_kernel, out_shape=(jax.ShapeDtypeStruct((rows, cols,...]
    dot_general x11 -> x0, matrix products: 65 us -> none  [the longest x2 19.5 us: ocean_mlp(): return jnp.dot(active, down_weight, preferred_element_type=jnp.float32)]
    gather x1 -> x0, local copies, waits for them, and re-layouts: 57.9 us -> none  [body(): picked = band_flat[overlay_cell_index].astype(jnp.float32)]
    transpose x4 -> x0, local copies, waits for them, and re-layouts: 29.5 us -> none  [the longest x3 19 us: to_windows(): return shaped.transpose(0, 2, 4, 1, 3, 5).reshape(-1, HEADS, WR * WC, HD)]
    reshape x7 -> x5, local copies, waits for them, and re-layouts: 30.8 us -> 1.55 us  [the longest x1 0.59 us: body(): head = jnp.pad(surface_temp_head, (0, pad)).reshape(2, LANES)]
    ppermute x16 -> x12, waiting for transfers between devices: 28.3 us -> 0.03 us  [the longest x1 0.01 us: body(): meta_west = lax.ppermute(meta[:, :, cols - HALO:], 'lon', right)]
    all_gather x1 -> x0, blocking collectives: 14.9 us -> none  [body(): band_flux = lax.all_gather(fluxes, 'lon', axis=1, tiled=True)]
  transfers between devices with their start and end apart: 16 -> 13, of which waited for: 11 -> 0; matrix products, arithmetic and copies ran while one was open for 8% -> 10% of each run, Pallas kernels for 0% -> 45%
where the time goes in v1:
time: 144 us; the launch traced here: 143 us
  Pallas kernels  86.7 us (60%)
  starting transfers between devices  33.5 us (23%)
  local copies, waits for them, and re-layouts  11.7 us (8%)
  other arithmetic  10.1 us (7%)
    pallas_call x1, Pallas kernels, ocean(): pl.pallas_call(ocean_kernel, out_shape=(jax.ShapeDtypeStruct((rows, cols,...  39.7 us
    pallas_call x2, Pallas kernels, atmosphere(): pl.pallas_call(functools.partial(atmosphere_kernel, is_edge), out_shape=(...  35.2 us
    ppermute x1, starting transfers between devices, body(): flux_north = lax.ppermute(flux[:, :run], 'lat', down_lat)  12.1 us
    pallas_call x1, Pallas kernels, regrid(): pl.pallas_call(functools.partial(regrid_kernel, band_cols, own_cols), out...  7.45 us
    pallas_call x1, Pallas kernels, update(): pl.pallas_call(update_kernel, grid=(rows // WR,), out_shape=jax.ShapeDtyp...  4.31 us
    ppermute x1, starting transfers between devices, body(): meta_east = lax.ppermute(meta[:, :, :HALO], 'lon', left)  4.1 us
    all_to_all x1, starting transfers between devices, body(): lax.all_to_all(jnp.broadcast_to(fluxes, (lon_count,) + fluxes.shape), 'lo...  3.98 us
    ppermute x1, starting transfers between devices, body(): east = lax.ppermute(ocean_features[:, :HALO], 'lon', left)  3.54 us
  transfers between devices with their start and end apart: 13, of which 0 were waited for; matrix products, arithmetic and copies ran while one was open for 10% of the time, Pallas kernels for 45%

profile of v1, /device:TPU:0, one launch (start us, length us, event | category | flops | bytes accessed | tf_op | source)
XLA Modules:
  0.0 143.0 jit_solution(13643146702592644196)
XLA Ops:
  0.6 1.1 convert_element_type.43
  1.7 0.8 convert_bitcast_fusion
  2.5 0.9 pad_maximum_fusion.6
  4.1 4.1 %collective-permute-start.8 = (f32[9,64,8]{2,1,0:T(8,128)S(1)}, f32[9,64,8]{2,1,0:T(8,128)S(1)}, u32[]{:S(2)}, u32[]{:S(2)}) collective-permute-start(f32[9,64,8]{2,1,0:T(8,128)S(1)} %get-tuple-element.25), channel_id=1, source_target_pairs={{0,7},{1,0},{2,1},{3,2},{4,3},{5,4},{6,5},{7,6},{8,15},{9,8},{10,9... | collective-permute-start | bytes 55304 | tf_op jit(solution)/shard_map/ppermute | solution.py:502
  8.2 1.0 slice.47.halo_ref
  10.0 0.8 fusion.6
  10.8 3.5 %collective-permute-start.3 = (bf16[64,8,192]{2,1,0:T(8,128)(2,1)}, bf16[64,8,192]{2,1,0:T(8,128)(2,1)S(1)}, u32[]{:S(2)}, u32[]{:S(2)}) collective-permute-start(bf16[64,8,192]{2,1,0:T(8,128)(2,1)} %get-tuple-element.18), channel_id=1, source_target_pairs={{0,7},{1,0},{2,1},{3,2},{4,3},{5,4},{6,5},{7,6},{8,15},{9,8},{10,9... | collective-permute-start | bytes 589832 | tf_op jit(solution)/shard_map/ppermute | solution.py:492
  15.8 1.3 pad_maximum_fusion.taps_ref
  19.0 0.9 collective-permute-start.9
  20.5 17.6 %atm_own.1 = (f32[512,768]{1,0:T(8,128)}, bf16[2,8,256]{2,1,0:T(8,128)(2,1)}) custom-call(bf16[32,32,768]{2,1,0:T(8,128)(2,1)} %x_ref.3, bf16[32,8,768]{2,1,0:T(8,128)(2,1)} %copy-done.1, f32[2,768]{1,0:T(2,128)} %pad_maximum_fusion.9.gains_ref, bf16[768,2304]{1,0:T(8,128)(2,1)} %wqkv_hbm.3, bf16[768,768]{1,0:T(8,128)(2,1)} %wout_hbm.3, ...), custom_call_target="tpu_custom_call" | custom-call | tf_op jit(solution)/shard_map/atm_own/pallas_call | solution.py:144
  38.7 0.8 pad_maximum_fusion.3.meta_ref
  40.2 17.6 %atm_edge.1 = (f32[512,768]{1,0:T(8,128)}, bf16[2,8,256]{2,1,0:T(8,128)(2,1)}) custom-call(bf16[32,32,768]{2,1,0:T(8,128)(2,1)} %x_ref.3, bf16[32,8,768]{2,1,0:T(8,128)(2,1)} %copy-done.9, f32[2,768]{1,0:T(2,128)} %pad_maximum_fusion.9.gains_ref, bf16[768,2304]{1,0:T(8,128)(2,1)} %wqkv_hbm.3, bf16[768,768]{1,0:T(8,128)(2,1)} %wout_hbm.3, ...), custom_call_target="tpu_custom_call" | custom-call | tf_op jit(solution)/shard_map/atm_edge/pallas_call | solution.py:144
  59.2 4.0 %all-to-all-start = ((bf16[8,4,8,256]{3,2,1,0:T(8,128)(2,1)}), bf16[8,4,8,256]{3,2,1,0:T(8,128)(2,1)S(1)}, u32[]{:S(2)}, u32[]{:S(2)}) async-start(bf16[8,4,8,256]{3,2,1,0:T(8,128)(2,1)} %broadcast_in_dim.12), calls=%async_computation | async-start | bytes 262144 | tf_op jit(solution)/shard_map/all_to_all | solution.py:531
  63.2 1.5 %collective-permute-start.4 = (bf16[8,80,192]{2,1,0:T(8,128)(2,1)S(1)}, bf16[8,80,192]{2,1,0:T(8,128)(2,1)S(1)}, u32[]{:S(2)}, u32[]{:S(2)}) collective-permute-start(bf16[8,80,192]{2,1,0:T(8,128)(2,1)S(1)} %pad_maximum_fusion.4), channel_id=1, source_target_pairs={{0,8},{8,16},{16,24},{24,0},{1,9},{9,17},{17,25},{25,1},{2,10},{10... | collective-permute-start | bytes 737288 | tf_op jit(solution)/shard_map/ppermute | solution.py:521
  64.8 3.3 %collective-permute-start.6 = (bf16[8,80,192]{2,1,0:T(8,128)(2,1)S(1)}, bf16[8,80,192]{2,1,0:T(8,128)(2,1)}, u32[]{:S(2)}, u32[]{:S(2)}) collective-permute-start(bf16[8,80,192]{2,1,0:T(8,128)(2,1)S(1)} %pad_maximum_fusion.4), channel_id=1, source_target_pairs={{0,7},{1,6},{2,5},{3,4},{4,3},{5,2},{6,1},{7,0},{8,15},{9,14},{10,... | collective-permute-start | bytes 737288 | tf_op jit(solution)/shard_map/ppermute | solution.py:522
  68.0 1.5 %convert.4 = bf16[512,768]{1,0:T(8,128)(2,1)S(1)} convert(f32[512,768]{1,0:T(8,128)} %get-tuple-element.9.edge_ref) | non-fusion elementwise | flops 393216 | bytes 2359296 | tf_op jit(solution)/shard_map/convert.1
  70.4 1.5 %collective-permute-start.5 = (bf16[8,80,192]{2,1,0:T(8,128)(2,1)S(1)}, bf16[8,80,192]{2,1,0:T(8,128)(2,1)}, u32[]{:S(2)}, u32[]{:S(2)}) collective-permute-start(bf16[8,80,192]{2,1,0:T(8,128)(2,1)S(1)} %pad_maximum_fusion.5), channel_id=1, source_target_pairs={{0,24},{8,0},{16,8},{24,16},{1,25},{9,1},{17,9},{25,17},{2,26},{10... | collective-permute-start | bytes 737288 | tf_op jit(solution)/shard_map/ppermute | solution.py:520
  72.5 7.5 %regrid.1.flux_ref = f32[16,5760]{1,0:T(8,128)} custom-call(bf16[32,8,256]{2,1,0:T(8,128)(2,1)} %bitcast.23, f32[9,5760]{1,0:T(8,128)} %pad_maximum_fusion.3.meta_ref), custom_call_target="tpu_custom_call" | custom-call | tf_op jit(solution)/shard_map/regrid/pallas_call | solution.py:217
  80.0 0.9 fusion.7
  81.4 12.1 %collective-permute-start.11 = (f32[16,640]{1,0:T(8,128)S(1)}, f32[16,640]{1,0:T(8,128)}, u32[]{:S(2)}, u32[]{:S(2)}) collective-permute-start(f32[16,640]{1,0:T(8,128)S(1)} %get-tuple-element.22), channel_id=1, source_target_pairs={{0,24},{8,0},{16,8},{24,16},{1,25},{9,1},{17,9},{25,17},{2,26},{10... | collective-permute-start | bytes 122888 | tf_op jit(solution)/shard_map/ppermute | solution.py:540
  94.4 1.1 pad.24.down_ref
  95.5 0.9 pad.23.up_ref
  98.2 39.7 %ocean.1 = (bf16[64,64,192]{2,1,0:T(8,128)(2,1)}, f32[32,32,128]{2,1,0:T(8,128)}) custom-call(f32[2]{0:T(128)} %add_convert_fusion.flags_ref, bf16[64,64,192]{2,1,0:T(8,128)(2,1)} %own_ref.1, bf16[64,8,192]{2,1,0:T(8,128)(2,1)} %copy-done.6, bf16[64,8,192]{2,1,0:T(8,128)(2,1)} %copy-done.7, bf16[8,80,192]{2,1,0:T(8,128)(2,1)} %copy-done.10, ...), custom_call_target="tpu_custom_call" | custom-call | tf_op jit(solution)/shard_map/ocean/pallas_call | solution.py:402
  138.7 4.3 %update.1 = bf16[32,32,768]{2,1,0:T(8,128)(2,1)} custom-call(f32[512,768]{1,0:T(8,128)} %get-tuple-element.8.own_ref, f32[512,768]{1,0:T(8,128)} %get-tuple-element.9.edge_ref, bf16[32,8,768]{2,1,0:T(8,128)(2,1)} %copy-done.8, f32[32,32,128]{2,1,0:T(8,128)} %get-tuple-element.12.sst_ref, f32[1,768]{1,0:T(1,128)} %broadcast_in_dim.33.embed_ref), custom_call_target="tpu_custom_call" | custom-call | tf_op jit(solution)/shard_map/update/pallas_call | solution.py:439
  (96 shorter events, 13.3 us)
Async XLA Ops:
  0.6 9.4 %copy-start = (bf16[64,64,192]{2,1,0:T(8,128)(2,1)S(1)}, bf16[64,64,192]{2,1,0:T(8,128)(2,1)}, u32[]{:S(2)}) copy-start(bf16[64,64,192]{2,1,0:T(8,128)(2,1)} %own_ref.1) | copy-start | bytes 4718596
  3.6 11.5 %copy-start.15 = (f32[768]{0:T(1024)S(1)}, f32[768]{0:T(1024)}, u32[]{:S(2)}) copy-start(f32[768]{0:T(1024)} %param.28) | copy-start | bytes 9220
  3.6 11.5 %copy-start.16 = (f32[768]{0:T(1024)S(1)}, f32[768]{0:T(1024)}, u32[]{:S(2)}) copy-start(f32[768]{0:T(1024)} %param.29) | copy-start | bytes 9220
  3.6 11.5 %copy-start.11 = (f32[2,49,192]{2,0,1:T(2,128)S(1)}, f32[2,49,192]{2,0,1:T(2,128)}, u32[]{:S(2)}) copy-start(f32[2,49,192]{2,0,1:T(2,128)} %param.33) | copy-start | bytes 225796
  3.6 14.9 %collective-permute-start.7 = (f32[9,64,8]{2,1,0:T(8,128)S(1)}, f32[9,64,8]{2,1,0:T(8,128)S(1)}, u32[]{:S(2)}, u32[]{:S(2)}) collective-permute-start(f32[9,64,8]{2,1,0:T(8,128)S(1)} %get-tuple-element.24), channel_id=1, source_target_pairs={{0,1},{1,2},{2,3},{3,4},{4,5},{5,6},{6,7},{7,0},{8,9},{9,10},{10,1... | collective-permute-start | bytes 55304 | tf_op jit(solution)/shard_map/ppermute | solution.py:501
  4.1 11.3 %copy-start.13 = (f32[8,192]{1,0:T(8,128)S(1)}, f32[8,192]{1,0:T(8,128)}, u32[]{:S(2)}) copy-start(f32[8,192]{1,0:T(8,128)} %param.32) | copy-start | bytes 18436
  4.1 14.4 %collective-permute-start.8 = (f32[9,64,8]{2,1,0:T(8,128)S(1)}, f32[9,64,8]{2,1,0:T(8,128)S(1)}, u32[]{:S(2)}, u32[]{:S(2)}) collective-permute-start(f32[9,64,8]{2,1,0:T(8,128)S(1)} %get-tuple-element.25), channel_id=1, source_target_pairs={{0,7},{1,0},{2,1},{3,2},{4,3},{5,4},{6,5},{7,6},{8,15},{9,8},{10,9... | collective-permute-start | bytes 55304 | tf_op jit(solution)/shard_map/ppermute | solution.py:502
  9.3 30.2 %collective-permute-start = (bf16[32,8,768]{2,1,0:T(8,128)(2,1)S(1)}, bf16[32,8,768]{2,1,0:T(8,128)(2,1)S(1)}, u32[]{:S(2)}, u32[]{:S(2)}) collective-permute-start(bf16[32,8,768]{2,1,0:T(8,128)(2,1)S(1)} %slice.47.halo_ref), channel_id=1, source_target_pairs={{0,7},{1,0},{2,1},{3,2},{4,3},{5,4},{6,5},{7,6},{8,15},{9,8},{10,9... | collective-permute-start | bytes 1179656 | tf_op jit(solution)/shard_map/ppermute | solution.py:490
  10.8 28.6 %collective-permute-start.2 = (bf16[64,8,192]{2,1,0:T(8,128)(2,1)}, bf16[64,8,192]{2,1,0:T(8,128)(2,1)S(1)}, u32[]{:S(2)}, u32[]{:S(2)}) collective-permute-start(bf16[64,8,192]{2,1,0:T(8,128)(2,1)} %get-tuple-element.19), channel_id=1, source_target_pairs={{0,1},{1,2},{2,3},{3,4},{4,5},{5,6},{6,7},{7,0},{8,9},{9,10},{10,1... | collective-permute-start | bytes 589832 | tf_op jit(solution)/shard_map/ppermute | solution.py:491
  10.8 28.6 %collective-permute-start.3 = (bf16[64,8,192]{2,1,0:T(8,128)(2,1)}, bf16[64,8,192]{2,1,0:T(8,128)(2,1)S(1)}, u32[]{:S(2)}, u32[]{:S(2)}) collective-permute-start(bf16[64,8,192]{2,1,0:T(8,128)(2,1)} %get-tuple-element.18), channel_id=1, source_target_pairs={{0,7},{1,0},{2,1},{3,2},{4,3},{5,4},{6,5},{7,6},{8,15},{9,8},{10,9... | collective-permute-start | bytes 589832 | tf_op jit(solution)/shard_map/ppermute | solution.py:492
  19.0 19.1 %collective-permute-start.9 = (f32[9,640]{1,0:T(8,128)S(1)}, f32[9,640]{1,0:T(8,128)S(1)}, u32[]{:S(2)}, u32[]{:S(2)}) collective-permute-start(f32[9,640]{1,0:T(8,128)S(1)} %slice.69), channel_id=1, source_target_pairs={{0,7},{1,6},{2,5},{3,4},{4,3},{5,2},{6,1},{7,0},{8,15},{9,14},{10,... | collective-permute-start | bytes 69128 | tf_op jit(solution)/shard_map/ppermute | solution.py:526
  39.4 18.4 %copy-start.6 = (bf16[64,8,192]{2,1,0:T(8,128)(2,1)}, bf16[64,8,192]{2,1,0:T(8,128)(2,1)S(1)}, u32[]{:S(2)}) copy-start(bf16[64,8,192]{2,1,0:T(8,128)(2,1)S(1)} %collective-permute-done.2.west_ref) | copy-start | bytes 589828
  39.4 18.4 %copy-start.7 = (bf16[64,8,192]{2,1,0:T(8,128)(2,1)}, bf16[64,8,192]{2,1,0:T(8,128)(2,1)S(1)}, u32[]{:S(2)}) copy-start(bf16[64,8,192]{2,1,0:T(8,128)(2,1)S(1)} %collective-permute-done.3.east_ref) | copy-start | bytes 589828
  39.5 18.4 %copy-start.14 = (bf16[2,8,256]{2,1,0:T(8,128)(2,1)S(1)}, bf16[2,8,256]{2,1,0:T(8,128)(2,1)}, u32[]{:S(2)}) copy-start(bf16[2,8,256]{2,1,0:T(8,128)(2,1)} %get-tuple-element.10) | copy-start | bytes 24580
  59.2 12.6 %all-to-all-start = ((bf16[8,4,8,256]{3,2,1,0:T(8,128)(2,1)}), bf16[8,4,8,256]{3,2,1,0:T(8,128)(2,1)S(1)}, u32[]{:S(2)}, u32[]{:S(2)}) async-start(bf16[8,4,8,256]{3,2,1,0:T(8,128)(2,1)} %broadcast_in_dim.12), calls=%async_computation | async-start | bytes 262144 | tf_op jit(solution)/shard_map/all_to_all | solution.py:531
  63.2 18.2 %collective-permute-start.4 = (bf16[8,80,192]{2,1,0:T(8,128)(2,1)S(1)}, bf16[8,80,192]{2,1,0:T(8,128)(2,1)S(1)}, u32[]{:S(2)}, u32[]{:S(2)}) collective-permute-start(bf16[8,80,192]{2,1,0:T(8,128)(2,1)S(1)} %pad_maximum_fusion.4), channel_id=1, source_target_pairs={{0,8},{8,16},{16,24},{24,0},{1,9},{9,17},{17,25},{25,1},{2,10},{10... | collective-permute-start | bytes 737288 | tf_op jit(solution)/shard_map/ppermute | solution.py:521
  64.8 32.8 %collective-permute-start.6 = (bf16[8,80,192]{2,1,0:T(8,128)(2,1)S(1)}, bf16[8,80,192]{2,1,0:T(8,128)(2,1)}, u32[]{:S(2)}, u32[]{:S(2)}) collective-permute-start(bf16[8,80,192]{2,1,0:T(8,128)(2,1)S(1)} %pad_maximum_fusion.4), channel_id=1, source_target_pairs={{0,7},{1,6},{2,5},{3,4},{4,3},{5,2},{6,1},{7,0},{8,15},{9,14},{10,... | collective-permute-start | bytes 737288 | tf_op jit(solution)/shard_map/ppermute | solution.py:522
  69.5 24.6 %copy-start.3 = (bf16[2,768,192]{1,2,0:T(8,128)(2,1)S(1)}, bf16[2,768,192]{1,2,0:T(8,128)(2,1)}, u32[]{:S(2)}) copy-start(bf16[2,768,192]{1,2,0:T(8,128)(2,1)} %param.36) | copy-start | bytes 1769476
  69.6 68.3 %collective-permute-start.1 = (bf16[32,8,768]{2,1,0:T(8,128)(2,1)S(1)}, bf16[32,8,768]{2,1,0:T(8,128)(2,1)S(1)}, u32[]{:S(2)}, u32[]{:S(2)}) collective-permute-start(bf16[32,8,768]{2,1,0:T(8,128)(2,1)S(1)} %slice.62), channel_id=1, source_target_pairs={{0,1},{1,2},{2,3},{3,4},{4,5},{5,6},{6,7},{7,0},{8,9},{9,10},{10,1... | collective-permute-start | bytes 1179656 | tf_op jit(solution)/shard_map/ppermute | solution.py:535
  70.4 27.2 %collective-permute-start.5 = (bf16[8,80,192]{2,1,0:T(8,128)(2,1)S(1)}, bf16[8,80,192]{2,1,0:T(8,128)(2,1)}, u32[]{:S(2)}, u32[]{:S(2)}) collective-permute-start(bf16[8,80,192]{2,1,0:T(8,128)(2,1)S(1)} %pad_maximum_fusion.5), channel_id=1, source_target_pairs={{0,24},{8,0},{16,8},{24,16},{1,25},{9,1},{17,9},{25,17},{2,26},{10... | collective-permute-start | bytes 737288 | tf_op jit(solution)/shard_map/ppermute | solution.py:520
  80.0 15.5 %copy-start.2 = (bf16[2,192,768]{2,1,0:T(8,128)(2,1)S(1)}, bf16[2,192,768]{2,1,0:T(8,128)(2,1)}, u32[]{:S(2)}) copy-start(bf16[2,192,768]{2,1,0:T(8,128)(2,1)} %param.35) | copy-start | bytes 1769476
  80.8 16.7 %collective-permute-start.10 = (f32[16,640]{1,0:T(8,128)S(1)}, f32[16,640]{1,0:T(8,128)S(1)}, u32[]{:S(2)}, u32[]{:S(2)}) collective-permute-start(f32[16,640]{1,0:T(8,128)S(1)} %get-tuple-element.23), channel_id=1, source_target_pairs={{0,8},{8,16},{16,24},{24,0},{1,9},{9,17},{17,25},{25,1},{2,10},{10... | collective-permute-start | bytes 122888 | tf_op jit(solution)/shard_map/ppermute | solution.py:541
  81.4 12.1 %copy-start.10 = (bf16[8,80,192]{2,1,0:T(8,128)(2,1)}, bf16[8,80,192]{2,1,0:T(8,128)(2,1)S(1)}, u32[]{:S(2)}) copy-start(bf16[8,80,192]{2,1,0:T(8,128)(2,1)S(1)} %collective-permute-done.4.south_ref) | copy-start | bytes 737284
  81.4 16.2 %collective-permute-start.11 = (f32[16,640]{1,0:T(8,128)S(1)}, f32[16,640]{1,0:T(8,128)}, u32[]{:S(2)}, u32[]{:S(2)}) collective-permute-start(f32[16,640]{1,0:T(8,128)S(1)} %get-tuple-element.22), channel_id=1, source_target_pairs={{0,24},{8,0},{16,8},{24,16},{1,25},{9,1},{17,9},{25,17},{2,26},{10... | collective-permute-start | bytes 122888 | tf_op jit(solution)/shard_map/ppermute | solution.py:540
  (9 other events, 19.1 us)
